TPU v7x, 128 devices: a whole 4x4x4 slice. The times are simulated.
128 devices in a mesh: wide: 32 (over x, z, core), narrow: 4 (over y).
Axes of the slice: x: 4, y: 4, z: 4, core: 2. Of those that a mesh axis runs over, the one named last changes fastest.
Arguments:
- table: bfloat16 [131072, 512], P(('wide', 'narrow')), may hold values from -1.5 to 1.5
- relations: bfloat16 [7424, 512], replicated, may hold values from -6 to 6
- req_rows: int32 [128, 2048], P(('wide', 'narrow')), may hold values from 0 to 1023, as said below
- owner_count: int32 [128, 128], P(('wide', 'narrow')), may hold values from 1 to 16, as said below
- owner_start: int32 [128, 128], P(('wide', 'narrow')), may hold values from 0 to 2032, as said below
- head_slot: int32 [131072], P(('wide', 'narrow')), may hold values from 0 to 2047, as said below
- rel_id: int32 [131072], P(('wide', 'narrow')), may hold values from 0 to 7423
- tail_slot: int32 [131072], P(('wide', 'narrow')), may hold values from 0 to 2047, as said below
- neg_slot: int32 [131072], P(('wide', 'narrow')), may hold values from 0 to 2047, as said below
Outputs:
- table_grad: float32 [131072, 512], P(('wide', 'narrow'))
Inputs may be any that keep to these rules, and one draw needn't show every extreme that they name: `req_rows`: entries past the device's total of owner_count are ignored. A row may be asked more than once by one device of one owner; the gradients of all its slots add. `owner_count`: in every draw some owners receive exactly 16 rows from every device, and some device asks 16 rows of every owner. `owner_start`: the running sum of owner_count along owners, starting at 0. `head_slot`: below the device's total of owner_count. `tail_slot`: below the device's total of owner_count. `neg_slot`: below the device's total of owner_count.
All inputs are finite; a program needn't handle non-finite values.
Results may differ from a plain program's by a relative error of at most 0.0065.
Values may be sent and summed in bfloat16 or wider, within the bound.
A program may use at most 64 MiB of HBM per device.

v0:
```python
import jax
import jax.numpy as jnp
from jax import lax
from jax.sharding import PartitionSpec as P


def locate(slot_ids, start, count, cap):
    owners = start.shape[0]
    offset = slot_ids[:, None] - start[None, :]
    match = (offset >= 0) & (offset < count[None, :])
    owner_ids = jnp.arange(owners, dtype=jnp.int32)
    flat = jnp.sum(jnp.where(match, owner_ids[None, :] * cap + offset, 0), axis=1)
    valid = jnp.any(match, axis=1)
    return (flat, valid)


def spread_sum(selector, values):
    upper = values.astype(jnp.bfloat16)
    lower = (values - upper.astype(jnp.float32)).astype(jnp.bfloat16)
    dims = (((0,), (0,)), ((), ()))
    first = lax.dot_general(selector, upper, dims, preferred_element_type=jnp.float32)
    second = lax.dot_general(selector, lower, dims, preferred_element_type=jnp.float32)
    return first + second


def slot_gradients(rows, flat, valid, rel_rows, batch):
    slot_ids = jnp.arange(rows.shape[0], dtype=jnp.int32)
    picker = ((flat[:, None] == slot_ids[None, :]) & valid[:, None]).astype(jnp.bfloat16)
    emb = jnp.dot(picker, rows, preferred_element_type=jnp.float32).astype(jnp.bfloat16)
    head = emb[:batch]
    tail = emb[batch : 2 * batch]
    negative = emb[2 * batch :]
    rvec = rel_rows.astype(jnp.float32)
    query = head.astype(jnp.float32) * rvec
    query_half = query.astype(jnp.bfloat16)
    positive = jnp.sum(query * tail.astype(jnp.float32), axis=1)
    negative_score = lax.dot_general(
        query_half, negative, (((1,), (1,)), ((), ())), preferred_element_type=jnp.float32
    )
    pos_weight = -jax.nn.sigmoid(-positive)
    neg_weight = jax.nn.sigmoid(negative_score).astype(jnp.bfloat16)
    head_grad = rvec * (
        pos_weight[:, None] * tail.astype(jnp.float32)
        + jnp.dot(neg_weight, negative, preferred_element_type=jnp.float32)
    )
    tail_grad = pos_weight[:, None] * query
    neg_grad = lax.dot_general(
        neg_weight, query_half, (((0,), (0,)), ((), ())), preferred_element_type=jnp.float32
    )
    per_row = jnp.concatenate([head_grad, tail_grad, neg_grad], axis=0)
    return spread_sum(picker, per_row)


def per_device(
    table, relations, req_rows, owner_count, owner_start, head_slot, rel_id, tail_slot, neg_slot
):
    n_wide = lax.axis_size("wide")
    n_narrow = lax.axis_size("narrow")
    owners = n_wide * n_narrow
    slots = req_rows.shape[1]
    cap = slots // owners
    width = table.shape[1]
    batch = head_slot.shape[0]
    count = owner_count[0]
    start = owner_start[0]
    packed = req_rows[0]
    column = jnp.arange(cap, dtype=jnp.int32)
    live = column[None, :] < count[:, None]
    where_at = jnp.clip(start[:, None] + column[None, :], 0, slots - 1)
    bucket = jnp.where(live, jnp.take(packed, where_at), 0)
    wanted = lax.all_to_all(bucket, ("wide", "narrow"), split_axis=0, concat_axis=0, tiled=True)
    found = jnp.take(table, wanted, axis=0)
    rows = lax.all_to_all(found, ("wide", "narrow"), split_axis=0, concat_axis=0, tiled=True)
    flat_rows = jnp.where(
        live.reshape(-1, 1), rows.reshape(owners * cap, width), jnp.zeros((), jnp.bfloat16)
    )
    lookups = jnp.concatenate([head_slot, tail_slot, neg_slot])
    flat, valid = locate(lookups, start, count, cap)
    rel_rows = jnp.take(relations, rel_id, axis=0)
    grads = slot_gradients(flat_rows, flat, valid, rel_rows, batch)
    back = lax.all_to_all(
        grads.reshape(owners, cap, width),
        ("wide", "narrow"),
        split_axis=0,
        concat_axis=0,
        tiled=True,
    )
    row_ids = jnp.arange(table.shape[0], dtype=jnp.int32)
    placer = (wanted.reshape(-1)[:, None] == row_ids[None, :]).astype(jnp.bfloat16)
    return spread_sum(placer, back.reshape(owners * cap, width))


def solution(mesh):
    in_specs = (
        P(("wide", "narrow"), None),
        P(),
        P(("wide", "narrow"), None),
        P(("wide", "narrow"), None),
        P(("wide", "narrow"), None),
        P(("wide", "narrow")),
        P(("wide", "narrow")),
        P(("wide", "narrow")),
        P(("wide", "narrow")),
    )
    out_specs = P(("wide", "narrow"), None)
    return jax.shard_map(
        per_device, mesh=mesh, in_specs=in_specs, out_specs=out_specs, check_vma=False
    )
```

profile of v0, /device:TPU:1, one launch (start us, length us, event | category | flops | bytes accessed | tf_op | source)
XLA Modules:
  0.0 192.5 jit_solution(17334405114817714912)
XLA Ops:
  0.0 0.0 copy-start
  0.0 0.8 compare_select_fusion.2
  0.9 0.1 reshape.249
  0.9 0.0 copy-done.1
  1.0 0.0 copy-start.4
  1.0 0.0 copy-start.5
  1.0 11.8 %gather_fusion = s32[2048]{0:T(1024)S(1)} fusion(s32[2048]{0:T(1024)S(1)} %bitcast.25, s32[2048]{0:T(1024)S(1)} %broadcast_clamp_fusion.1), kind=kCustom, calls=%fused_computation | custom fusion | bytes 24576 | tf_op jit(solution)/shard_map/jit(_take)/gather | solution.py:70
  12.8 0.1 gather.15
  12.8 0.0 copy-done.4
  12.9 0.0 copy-done.5
  12.9 0.1 select_select_fusion
  13.0 21.2 %all_to_all.22 = s32[128,1,16]{2,1,0:T(1,128)S(1)} all-to-all(s32[128,1,16]{2,1,0:T(1,128)S(1)} %bitcast.30), channel_id=1, replica_groups=mesh['wide'=32,'narrow'=4] {'wide','narrow'}, dimensions={0} | all-to-all | bytes 16384 | tf_op jit(solution)/shard_map/all_to_all | solution.py:71
  34.2 0.1 reshape.265
  34.3 0.0 copy-done
  34.3 7.5 %gather_fusion.2 = bf16[2048,512]{1,0:T(8,128)(2,1)S(1)} fusion(bf16[1024,512]{1,0:T(8,128)(2,1)S(1)} %copy-done, s32[2048]{0:T(1024)S(1)} %broadcast_clamp_fusion), kind=kCustom, calls=%fused_computation.2 | custom fusion | bytes 4202496 | tf_op jit(solution)/shard_map/jit(_take)/gather | solution.py:72
  41.9 1.5 broadcast_select_fusion
  43.4 5.0 %all-to-all-start.1 = ((bf16[128,16,512]{2,1,0:T(8,128)(2,1)}), bf16[128,16,512]{2,1,0:T(8,128)(2,1)}, u32[]{:S(2)}, u32[]{:S(2)}) async-start(bf16[128,16,512]{2,1,0:T(8,128)(2,1)} %broadcast_select_fusion), calls=%async_computation.1 | async-start | bytes 4194304 | tf_op jit(solution)/shard_map/all_to_all | solution.py:73
  48.4 0.1 iota_compare_fusion.6
  48.5 0.1 lt.111
  48.6 0.0 copy-done.3
  48.6 0.0 copy-start.6
  48.7 0.0 copy-start.7
  48.7 0.0 copy-start.8
  48.7 8.1 %gather_fusion.1 = bf16[1024,512]{1,0:T(8,128)(2,1)S(1)} fusion(bf16[7424,512]{1,0:T(8,128)(2,1)} %param.10, s32[1024]{0:T(1024)S(1)} %fusion.44), kind=kCustom, calls=%fused_computation.1 | custom fusion | bytes 2101248 | tf_op jit(solution)/shard_map/jit(_take)/gather | solution.py:79
  56.8 0.0 copy-done.6
  56.9 0.0 copy-done.7
  56.9 0.0 copy-done.8
  56.9 1.9 fusion.37
  58.8 1.9 fusion.32
  60.7 18.5 %all-to-all-done.1 = bf16[128,16,512]{2,1,0:T(8,128)(2,1)} async-done(((bf16[128,16,512]{2,1,0:T(8,128)(2,1)}), bf16[128,16,512]{2,1,0:T(8,128)(2,1)}, u32[]{:S(2)}, u32[]{:S(2)}) %all-to-all-start.1) | async-done | bytes 2097184 | tf_op jit(solution)/shard_map/all_to_all | solution.py:73
  79.2 1.8 bitcast_select_fusion
  81.0 8.7 %fusion.15 = bf16[3072,512]{1,0:T(8,128)(2,1)S(1)} fusion(bf16[2048,512]{1,0:T(8,128)(2,1)S(1)} %bitcast_select_fusion, s32[3072]{0:T(1024)S(1)} %fusion.32, pred[3072]{0:T(1024)(128)(4,1)S(1)} %fusion.37), kind=kOutput, calls=%fused_computation.19 | convolution fusion | flops 6456606720 | bytes 5258240 | tf_op jit(solution)/shard_map/dot_general | solution.py:29
  89.7 0.8 fusion.27
  90.5 2.5 %divide_convert_fusion = bf16[1024,1024]{1,0:T(8,128)(2,1)S(1)} fusion(bf16[3072,512]{1,0:T(8,128)(2,1)S(1)} %fusion.15, bf16[1024,512]{1,0:T(8,128)(2,1)S(1)} %gather_fusion.1, pred[1024]{0:T(1024)(128)(4,1)S(1)} %compare_and_fusion.1), kind=kOutput, calls=%fused_computation.24 | convolution fusion | flops 1080557568 | bytes 5243904 | tf_op jit(solution)/shard_map/dot_general | solution.py:37
  93.0 0.5 fusion.29
  93.5 2.7 %convert_multiply_fusion.2 = f32[1024,512]{1,0:T(8,128)} fusion(bf16[1024,1024]{1,0:T(8,128)(2,1)S(1)} %divide_convert_fusion, f32[1024]{0:T(1024)S(1)} %divide_negate_fusion, bf16[3072,512]{1,0:T(8,128)(2,1)S(1)} %fusion.15, bf16[1024,512]{1,0:T(8,128)(2,1)S(1)} %gather_fusion.1, pred[1024]{0:T(1024)(128)(4,1)S(1)} %compare_and_fusion.1), kind=kOutput, calls=%fused_computation.33 | convolution fusion | flops 1076887552 | bytes 7345152 | tf_op jit(solution)/shard_map/dot_general | solution.py:44
  96.3 1.4 fusion.38
  97.7 1.3 copy-done.9
  99.0 11.4 %fusion.3 = f32[2048,512]{1,0:T(8,128)} fusion(s32[3072]{0:T(1024)S(1)} %fusion.32, pred[3072]{0:T(1024)(128)(4,1)S(1)} %fusion.37, f32[1024,512]{1,0:T(8,128)S(1)} %fusion.38, f32[1024,512]{1,0:T(8,128)S(1)} %fusion.29, f32[1024,512]{1,0:T(8,128)} %convert_multiply_fusion.2), kind=kOutput, calls=%fused_computation.6 | convolution fusion | flops 6464471040 | bytes 10501120 | tf_op jit(solution)/shard_map/dot_general | solution.py:21
  110.4 14.3 %fusion.22 = f32[2048,512]{1,0:T(8,128)} fusion(f32[2048,512]{1,0:T(8,128)} %fusion.3, f32[1024,512]{1,0:T(8,128)} %copy-done.9, f32[1024,512]{1,0:T(8,128)} %copy-done.2, f32[1024,512]{1,0:T(8,128)} %convert_multiply_fusion.2, s32[3072]{0:T(1024)S(1)} %fusion.32, pred[3072]{0:T(1024)(128)(4,1)S(1)} %fusion.37), kind=kOutput, calls=%fused_computation.27 | convolution fusion | flops 6465519616 | bytes 14695424 | tf_op jit(solution)/shard_map/dot_general | solution.py:22
  124.7 5.0 %all-to-all-start.2 = ((f32[128,16,512]{2,1,0:T(8,128)}), f32[128,16,512]{2,1,0:T(8,128)}, u32[]{:S(2)}, u32[]{:S(2)}) async-start(f32[128,16,512]{2,1,0:T(8,128)} %bitcast.27), calls=%async_computation.2 | async-start | bytes 8388608 | tf_op jit(solution)/shard_map/all_to_all | solution.py:81
  129.8 0.5 broadcast.228
  130.3 0.8 reduce.3
  131.1 0.1 eq.28
  131.2 51.5 %all-to-all-done.2 = f32[128,16,512]{2,1,0:T(8,128)} async-done(((f32[128,16,512]{2,1,0:T(8,128)}), f32[128,16,512]{2,1,0:T(8,128)}, u32[]{:S(2)}, u32[]{:S(2)}) %all-to-all-start.2) | async-done | bytes 4194336 | tf_op jit(solution)/shard_map/all_to_all | solution.py:81
  182.7 2.8 %fusion.19 = (bf16[2048,512]{1,0:T(8,128)(2,1)S(1)}, bf16[2048,512]{1,0:T(8,128)(2,1)S(1)}) fusion(f32[128,16,512]{2,1,0:T(8,128)} %all-to-all-done.2), kind=kLoop, calls=%fused_computation.23 | loop fusion | flops 4194304 | bytes 8388608 | tf_op jit(solution)/shard_map/convert_element_type | solution.py:19
  185.5 2.8 %fusion.13 = f32[1024,512]{1,0:T(8,128)S(1)} fusion(bf16[2048,512]{1,0:T(8,128)(2,1)S(1)} %get-tuple-element.5, s32[2048]{0:T(1024)S(1)} %eq.28), kind=kOutput, calls=%fused_computation.15 | convolution fusion | flops 2149580800 | bytes 4202496 | tf_op jit(solution)/shard_map/dot_general | solution.py:22
  188.3 4.1 %fusion.34 = f32[1024,512]{1,0:T(8,128)} fusion(f32[1024,512]{1,0:T(8,128)S(1)} %fusion.13, bf16[2048,512]{1,0:T(8,128)(2,1)S(1)} %get-tuple-element.6, s32[2048]{0:T(1024)S(1)} %eq.28), kind=kOutput, calls=%fused_computation.44 | convolution fusion | flops 2150105088 | bytes 6299648 | tf_op jit(solution)/shard_map/dot_general | solution.py:21
  (14 shorter events, 0.1 us)
Async XLA Ops:
  0.0 34.3 %copy-start = (bf16[1024,512]{1,0:T(8,128)(2,1)S(1)}, bf16[1024,512]{1,0:T(8,128)(2,1)}, u32[]{:S(2)}) copy-start(bf16[1024,512]{1,0:T(8,128)(2,1)} %param.9) | copy-start | bytes 3145732
  0.0 0.9 copy-start.1
  1.0 11.9 %copy-start.4 = (s32[1,128]{1,0:T(1,128)S(1)}, s32[1,128]{1,0:T(1,128)}, u32[]{:S(2)}) copy-start(s32[1,128]{1,0:T(1,128)} %param.13) | copy-start | bytes 1540
  1.0 11.9 %copy-start.5 = (s32[1,128]{1,0:T(1,128)S(1)}, s32[1,128]{1,0:T(1,128)}, u32[]{:S(2)}) copy-start(s32[1,128]{1,0:T(1,128)} %param.12) | copy-start | bytes 1540
  43.4 5.2 %copy-start.3 = (s32[1024]{0:T(1024)S(1)}, s32[1024]{0:T(1024)}, u32[]{:S(2)}) copy-start(s32[1024]{0:T(1024)} %param.15) | copy-start | bytes 12292
  43.4 35.8 %all-to-all-start.1 = ((bf16[128,16,512]{2,1,0:T(8,128)(2,1)}), bf16[128,16,512]{2,1,0:T(8,128)(2,1)}, u32[]{:S(2)}, u32[]{:S(2)}) async-start(bf16[128,16,512]{2,1,0:T(8,128)(2,1)} %broadcast_select_fusion), calls=%async_computation.1 | async-start | bytes 4194304 | tf_op jit(solution)/shard_map/all_to_all | solution.py:73
  48.6 8.2 %copy-start.6 = (s32[1024]{0:T(1024)S(1)}, s32[1024]{0:T(1024)}, u32[]{:S(2)}) copy-start(s32[1024]{0:T(1024)} %param.17) | copy-start | bytes 12292
  48.7 8.2 %copy-start.7 = (s32[1024]{0:T(1024)S(1)}, s32[1024]{0:T(1024)}, u32[]{:S(2)}) copy-start(s32[1024]{0:T(1024)} %param.16) | copy-start | bytes 12292
  48.7 8.2 %copy-start.8 = (s32[1024]{0:T(1024)S(1)}, s32[1024]{0:T(1024)}, u32[]{:S(2)}) copy-start(s32[1024]{0:T(1024)} %param.14) | copy-start | bytes 12292
  93.5 4.2 %copy-start.2 = (f32[1024,512]{1,0:T(8,128)}, f32[1024,512]{1,0:T(8,128)S(1)}, u32[]{:S(2)}) copy-start(f32[1024,512]{1,0:T(8,128)S(1)} %fusion.29) | copy-start | bytes 6291460
  97.7 1.3 copy-start.9
  124.7 57.9 %all-to-all-start.2 = ((f32[128,16,512]{2,1,0:T(8,128)}), f32[128,16,512]{2,1,0:T(8,128)}, u32[]{:S(2)}, u32[]{:S(2)}) async-start(f32[128,16,512]{2,1,0:T(8,128)} %bitcast.27), calls=%async_computation.2 | async-start | bytes 8388608 | tf_op jit(solution)/shard_map/all_to_all | solution.py:81
where the time goes:
time: 193 us; the launch traced here: 192 us
  waiting for transfers between devices  70 us (36%)
  matrix products  48 us (25%)
  local copies, waits for them, and re-layouts  29.8 us (15%)
  blocking collectives  21.2 us (11%)
  other arithmetic  13.1 us (7%)
  starting transfers between devices  10 us (5%)
    all_to_all x1, waiting for transfers between devices, per_device(): lax.all_to_all(grads.reshape(owners, cap, width), ('wide', 'narrow'), spl...  51.5 us
    all_to_all x1, blocking collectives, per_device(): lax.all_to_all(bucket, ('wide', 'narrow'), split_axis=0, concat_axis=0, t...  21.2 us
    all_to_all x1, waiting for transfers between devices, per_device(): lax.all_to_all(found, ('wide', 'narrow'), split_axis=0, concat_axis=0, ti...  18.5 us
    dot_general x2, matrix products, spread_sum(): lax.dot_general(selector, lower, dims, preferred_element_type=jnp.float32)  17.1 us
    dot_general x2, matrix products, spread_sum(): lax.dot_general(selector, upper, dims, preferred_element_type=jnp.float32)  15.6 us
    gather x2, local copies, waits for them, and re-layouts, per_device(): bucket = jnp.where(live, jnp.take(packed, where_at), 0)  11.9 us
    dot_general x1, matrix products, slot_gradients(): jnp.dot(picker, rows, preferred_element_type=jnp.float32)  8.69 us
    gather x1, local copies, waits for them, and re-layouts, per_device(): rel_rows = jnp.take(relations, rel_id, axis=0)  8.14 us
  transfers between devices with their start and end apart: 2, of which 2 were waited for; matrix products, arithmetic and copies ran while one was open for 7% of the time, Pallas kernels for 0%

commit v1 on v0

v1 whole, which is shorter than its diff:
```python
import jax
import jax.numpy as jnp
from jax import lax
from jax.experimental import pallas as pl
from jax.experimental.pallas import tpu as pltpu
from jax.sharding import PartitionSpec as P

MESH = pl.DeviceIdType.MESH
CAP = 16
GROUP = 16
GROUPS = 8
SPAN = CAP * GROUP
LANES = 128
F32 = jnp.float32
BF16 = jnp.bfloat16


def onehot(match):
    return jnp.where(match, 1.0, 0.0).astype(BF16)


def column(row):
    return jnp.transpose(jnp.broadcast_to(row, (LANES, LANES)))


def iota(shape, axis):
    return lax.broadcasted_iota(jnp.int32, shape, axis)


def kernel(
    table_h, rel_h, req_h, count_h, start_h, head_h, relid_h, tail_h, neg_h,
    out_ref,
    table, rel, req, count, start, look, relid,
    slotrow, slotcol, reqrow, lookcol, relcol, lookrow,
    idxbuf, wantrow, found, rows, rvec, emb, negb, qhalf, nweight, perrow, sent, back,
    local_sem, id_send, id_recv, row_send, row_recv, grad_send, grad_recv,
):
    w = lax.axis_index("wide")
    y = lax.axis_index("narrow")
    x, z, core = w // 8, (w // 2) % 4, w % 2
    ahead = ([(x + d) % 4 * 8 for d in range(4)], [(z + d) % 4 * 2 for d in range(4)])
    behind = ([(x + 4 - d) % 4 * 8 for d in range(4)], [(z + 4 - d) % 4 * 2 for d in range(4)])

    def each_partner(g, forward, act):
        t, c = g // 2, g % 2
        cc = (core + c) % 2
        xs, zs = ahead if forward else behind
        if forward:
            ys = [(y + t + 8 - m) % 4 for m in range(4)]
        else:
            ys = [(y + 8 - t + m) % 4 for m in range(4)]
        for u in range(GROUP):
            dx, dz = u // 4, u % 4
            device = (xs[dx] + zs[dz] + cc, ys[(dx + dz) % 4])
            if u == 0:
                pl.when(g > 0)(lambda device=device: act(0, device))
            else:
                act(u, device)

    barrier = pltpu.get_barrier_semaphore()

    @pl.loop(0, GROUPS)
    def _(g):
        each_partner(
            g, True, lambda u, device: pl.semaphore_signal(barrier, inc=1, device_id=device, device_id_type=MESH)
        )

    loads = [
        (start_h, start), (count_h, count), (req_h, req),
        (head_h, look.at[pl.ds(0, 8)]), (tail_h, look.at[pl.ds(8, 8)]), (neg_h, look.at[pl.ds(16, 8)]),
        (relid_h, relid), (table_h, table), (rel_h, rel),
    ]
    copies = [pltpu.make_async_copy(a, b, local_sem.at[i]) for i, (a, b) in enumerate(loads)]
    for copy in copies:
        copy.start()
    for copy in copies[:7]:
        copy.wait()

    row16 = iota((16, LANES), 0)
    first, many = start[...], count[...]
    facts = jnp.where(row16 == 0, first >> 6, jnp.where(row16 == 1, first & 63, jnp.where(row16 == 2, many, 0)))
    facts = facts.astype(F32).astype(BF16)
    asked = req[...]
    digits = jnp.concatenate([asked >> 5, asked & 31], axis=0).astype(F32).astype(BF16)
    down = iota((LANES, LANES), 0)

    @pl.loop(0, 16)
    def _(r):
        lane = iota((1, LANES), 1)
        k = r * 8 + (lane >> 4)
        c = lane & 15
        t, cc, u = k >> 5, (k >> 4) & 1, k & 15
        dx, dz = u >> 2, u & 3
        dy = (t - dx - dz) & 3
        owner = ((((x + dx) & 3) * 4 + ((z + dz) & 3)) * 2 + ((core + cc) & 1)) * 4 + ((y + dy) & 3)
        known = jnp.dot(facts, onehot(down == owner), preferred_element_type=F32)
        slot = (known[0:1] * 64.0 + known[1:2]).astype(jnp.int32) + c
        live = c < known[2:3].astype(jnp.int32)
        place = jnp.where(live, slot, -1).astype(F32)
        slotrow[pl.ds(r, 1)] = place
        slotcol[pl.ds(pl.multiple_of(r * LANES, LANES), LANES)] = column(place)
        picked = jnp.dot(digits, onehot(down == (slot & 127)), preferred_element_type=F32)
        mine = row16 == (slot >> 7)
        high = jnp.sum(jnp.where(mine, picked[:16], 0.0), axis=0, keepdims=True)
        low = jnp.sum(jnp.where(mine, picked[16:], 0.0), axis=0, keepdims=True)
        reqrow[pl.ds(r, 1)] = jnp.where(live, high * 32.0 + low, 0.0)

    lookrow[...] = look[...].astype(F32)

    pl.semaphore_wait(barrier, GROUPS * GROUP - 1)

    @pl.loop(0, GROUPS)
    def _(g):
        def send(u, device):
            pltpu.make_async_remote_copy(
                src_ref=reqrow.at[pl.ds(g * 2 + u // 8, 1)],
                dst_ref=idxbuf.at[pl.ds(g * GROUP + u, 1)],
                send_sem=id_send,
                recv_sem=id_recv.at[g],
                device_id=device,
                device_id_type=MESH,
            ).start()

        each_partner(g, True, send)

    idxbuf[0:1] = reqrow[0:1]

    @pl.loop(0, 24)
    def _(i):
        lookcol[pl.ds(pl.multiple_of(i * LANES, LANES), LANES)] = column(lookrow[pl.ds(i, 1)])

    @pl.loop(0, 8)
    def _(i):
        relcol[pl.ds(pl.multiple_of(i * LANES, LANES), LANES)] = column(relid[pl.ds(i, 1)].astype(F32))

    copies[7].wait()
    some_device = (ahead[0][1] + ahead[1][0] + core, y)

    def arrived(buf, sem, g, unit):
        def wait(first, n):
            part = buf.at[pl.ds(pl.multiple_of(first * unit, unit), n * unit)]
            pltpu.make_async_remote_copy(
                src_ref=part, dst_ref=part, send_sem=sem.at[g], recv_sem=sem.at[g],
                device_id=some_device, device_id_type=MESH,
            ).wait_recv()

        pl.when(g == 0)(lambda: wait(1, GROUP - 1))
        pl.when(g > 0)(lambda: wait(g * GROUP, GROUP))

    def drained(buf, sem, unit):
        n = GROUPS * GROUP - 1
        part = buf.at[pl.ds(unit, n * unit)]
        pltpu.make_async_remote_copy(
            src_ref=part, dst_ref=part, send_sem=sem, recv_sem=sem, device_id=some_device, device_id_type=MESH
        ).wait_send()

    def send_blocks(src, dst, send_sem, recv_sem, g, forward):
        def send(u, device):
            at = pl.ds(pl.multiple_of((g * GROUP + u) * CAP, CAP), CAP)
            pltpu.make_async_remote_copy(
                src_ref=src.at[at], dst_ref=dst.at[at], send_sem=send_sem, recv_sem=recv_sem.at[g],
                device_id=device, device_id_type=MESH,
            ).start()

        each_partner(g, forward, send)

    @pl.loop(0, GROUPS)
    def _(g):
        arrived(idxbuf, id_recv, g, 1)
        belongs = (iota((8, LANES), 1) >> 4) == iota((8, LANES), 0)
        halves = []
        for h in range(2):
            got = idxbuf[pl.ds(pl.multiple_of(g * 16 + h * 8, 8), 8)]
            row = jnp.sum(jnp.where(belongs, got, 0.0), axis=0, keepdims=True)
            wantrow[pl.ds(g * 2 + h, 1)] = row
            halves.append(column(row).astype(jnp.int32))
        want = jnp.concatenate(halves, axis=0)
        across = iota((SPAN, LANES), 1)
        pick = jnp.concatenate([onehot(want == across + i * LANES) for i in range(8)], axis=1)
        here = jnp.dot(pick, table[...], preferred_element_type=F32).astype(BF16)
        found[pl.ds(pl.multiple_of(g * SPAN, SPAN), SPAN)] = here
        send_blocks(found, rows, row_send, row_recv, g, False)

    rows[0:CAP] = found[0:CAP]

    copies[8].wait()
    rvec[...] = jnp.zeros_like(rvec)

    @pl.loop(0, rel.shape[0] // 256)
    def _(q):
        across = (iota((1024, LANES), 1) + q * 256).astype(F32)
        ids = relcol[...]
        pick = jnp.concatenate([onehot(ids == across), onehot(ids == across + 128.0)], axis=1)
        rvec[...] += jnp.dot(pick, rel[pl.ds(pl.multiple_of(q * 256, 256), 256)], preferred_element_type=F32)

    emb[...] = jnp.zeros_like(emb)

    @pl.loop(0, GROUPS)
    def _(g):
        arrived(rows, row_recv, g, CAP)

        @pl.loop(0, 3)
        def _(b):
            at = pl.ds(pl.multiple_of(b * 1024, 1024), 1024)
            ids = lookcol[at]
            pick = jnp.concatenate([onehot(ids == slotrow[pl.ds(g * 2 + h, 1)]) for h in range(2)], axis=1)
            emb[at] += jnp.dot(pick, rows[pl.ds(pl.multiple_of(g * SPAN, SPAN), SPAN)], preferred_element_type=F32)

    negb[...] = emb[2048:].astype(BF16)

    @pl.loop(0, 4)
    def _(b):
        at = pl.ds(pl.multiple_of(b * 256, 256), 256)
        r = rvec[at]
        query = emb[at] * r
        half = query.astype(BF16)
        qhalf[at] = half
        tail = emb[pl.ds(pl.multiple_of(1024 + b * 256, 256), 256)]
        positive = jnp.sum(query * tail, axis=1, keepdims=True)
        pos_weight = -1.0 / (1.0 + jnp.exp(positive))
        perrow[pl.ds(pl.multiple_of(1024 + b * 256, 256), 256)] = (pos_weight * query).astype(BF16)
        score = lax.dot_general(half, negb[...], (((1,), (1,)), ((), ())), preferred_element_type=F32)
        weight = (1.0 / (1.0 + jnp.exp(-score))).astype(BF16)
        nweight[at] = weight
        pulled = jnp.dot(weight, negb[...], preferred_element_type=F32)
        perrow[at] = (r * (pos_weight * tail + pulled)).astype(BF16)

    perrow[2048:] = lax.dot_general(
        nweight[...], qhalf[...], (((0,), (0,)), ((), ())), preferred_element_type=F32
    ).astype(BF16)

    @pl.loop(0, GROUPS)
    def _(g):
        at = pl.ds(pl.multiple_of(g * SPAN, SPAN), SPAN)
        place = slotcol[at]
        pick = jnp.concatenate([onehot(place == lookrow[i : i + 1]) for i in range(24)], axis=1)
        sent[at] = jnp.dot(pick, perrow[...], preferred_element_type=F32).astype(BF16)
        send_blocks(sent, back, grad_send, grad_recv, g, True)

    back[0:CAP] = sent[0:CAP]
    out_ref[...] = jnp.zeros_like(out_ref)

    @pl.loop(0, GROUPS)
    def _(g):
        arrived(back, grad_recv, g, CAP)
        down = iota((1024, LANES), 0).astype(F32)
        pick = jnp.concatenate([onehot(down == wantrow[pl.ds(g * 2 + h, 1)]) for h in range(2)], axis=1)
        out_ref[...] += jnp.dot(
            pick, back[pl.ds(pl.multiple_of(g * SPAN, SPAN), SPAN)], preferred_element_type=F32
        )

    drained(idxbuf, id_send, 1)
    drained(found, row_send, CAP)
    drained(sent, grad_send, CAP)


def per_device(table, relations, req_rows, owner_count, owner_start, head_slot, rel_id, tail_slot, neg_slot):
    ents, width = table.shape
    slots = req_rows.shape[1]
    batch = head_slot.shape[0]
    vmem = pltpu.VMEM
    dma = pltpu.SemaphoreType.DMA
    scratch = [
        vmem((ents, width), BF16), vmem(relations.shape, BF16), vmem((16, LANES), jnp.int32),
        vmem((1, LANES), jnp.int32), vmem((1, LANES), jnp.int32), vmem((24, LANES), jnp.int32),
        vmem((8, LANES), jnp.int32),
        vmem((16, LANES), F32), vmem((slots, LANES), F32), vmem((16, LANES), F32),
        vmem((3 * batch, LANES), F32), vmem((batch, LANES), F32), vmem((24, LANES), F32),
        vmem((128, LANES), F32), vmem((16, LANES), F32), vmem((slots, width), BF16), vmem((slots, width), BF16),
        vmem((batch, width), F32), vmem((3 * batch, width), F32), vmem((batch, width), BF16),
        vmem((batch, width), BF16), vmem((batch, batch), BF16), vmem((3 * batch, width), BF16),
        vmem((slots, width), BF16), vmem((slots, width), BF16),
        dma((9,)), dma, dma((GROUPS,)), dma, dma((GROUPS,)), dma, dma((GROUPS,)),
    ]
    return pl.pallas_call(
        kernel,
        out_shape=jax.ShapeDtypeStruct((ents, width), F32),
        in_specs=[pl.BlockSpec(memory_space=pl.ANY)] * 9,
        out_specs=pl.BlockSpec(memory_space=pltpu.VMEM),
        scratch_shapes=scratch,
        compiler_params=pltpu.CompilerParams(
            collective_id=0, has_side_effects=True, vmem_limit_bytes=60 * 2**20
        ),
        name="distmult_step",
    )(
        table,
        relations,
        req_rows.reshape(16, LANES),
        owner_count,
        owner_start,
        head_slot.reshape(8, LANES),
        rel_id.reshape(8, LANES),
        tail_slot.reshape(8, LANES),
        neg_slot.reshape(8, LANES),
    )


def solution(mesh):
    both = ("wide", "narrow")
    in_specs = (P(both, None), P(), P(both, None), P(both, None), P(both, None), P(both), P(both), P(both), P(both))
    return jax.shard_map(per_device, mesh=mesh, in_specs=in_specs, out_specs=P(both, None), check_vma=False)
```

time: 193 us -> 83.5 us (0.43)
  Pallas kernels: 0 us -> 80.3 us
  waiting for transfers between devices: 70 us -> 0 us
  matrix products: 48 us -> 0 us
  local copies, waits for them, and re-layouts: 29.8 us -> 3.08 us
  blocking collectives: 21.2 us -> 0 us
  other arithmetic: 13.1 us -> 0 us
  starting transfers between devices: 10 us -> 0 us
    pallas_call x0 -> x1, Pallas kernels: none -> 80.3 us  [per_device(): pl.pallas_call(kernel, out_shape=jax.ShapeDtypeStruct((ents, width), F32)...]
    all_to_all x2 -> x0, waiting for transfers between devices: 70 us -> none  [the longest x1 51.5 us: per_device(): lax.all_to_all(grads.reshape(owners, cap, width), ('wide', 'narrow'), spl...]
    dot_general x8 -> x0, matrix products: 48 us -> none  [the longest x2 17.1 us: spread_sum(): lax.dot_general(selector, lower, dims, preferred_element_type=jnp.float32)]
    gather x4 -> x0, local copies, waits for them, and re-layouts: 27.5 us -> none  [the longest x2 11.9 us: per_device(): bucket = jnp.where(live, jnp.take(packed, where_at), 0)]
    all_to_all x1 -> x0, blocking collectives: 21.2 us -> none  [per_device(): lax.all_to_all(bucket, ('wide', 'narrow'), split_axis=0, concat_axis=0, t...]
    all_to_all x2 -> x0, starting transfers between devices: 10 us -> none  [the longest x1 5.02 us: per_device(): lax.all_to_all(grads.reshape(owners, cap, width), ('wide', 'narrow'), spl...]
    select_n x5 -> x0, other arithmetic: 4.26 us -> none  [the longest x1 1.77 us: per_device(): jnp.where(live.reshape(-1, 1), rows.reshape(owners * cap, width), jnp.zer...]
    convert_element_type x1 -> x0, other arithmetic: 2.82 us -> none  [spread_sum(): lower = (values - upper.astype(jnp.float32)).astype(jnp.bfloat16)]
  transfers between devices with their start and end apart: 2 -> 0, of which waited for: 2 -> 0; matrix products, arithmetic and copies ran while one was open for 7% -> 0% of each run, Pallas kernels for 0% -> 0%
where the time goes in v1:
time: 83.5 us; the launch traced here: 83.4 us
  Pallas kernels  80.3 us (96%)
  local copies, waits for them, and re-layouts  3.08 us (4%)
    pallas_call x1, Pallas kernels, per_device(): pl.pallas_call(kernel, out_shape=jax.ShapeDtypeStruct((ents, width), F32)...  80.3 us
    unnamed x1, local copies, waits for them, and re-layouts  3.08 us

profile of v1, /device:TPU:1, one launch (start us, length us, event | category | flops | bytes accessed | tf_op | source)
XLA Modules:
  0.0 83.4 jit_solution(9202997820538046195)
XLA Ops:
  0.0 80.3 %distmult_step.1 = f32[1024,512]{1,0:T(8,128)} custom-call(bf16[1024,512]{1,0:T(8,128)(2,1)} %table_h.1, bf16[7424,512]{1,0:T(8,128)(2,1)} %rel_h.1, s32[16,128]{1,0:T(8,128)} %bitcast.5, s32[1,128]{1,0:T(1,128)} %count_h.1, s32[1,128]{1,0:T(1,128)} %start_h.1, s32[8,128]{1,0:T(8,128)} %bitcast.6, s32[8,128]{1,0:T(8,128)} %bitcast.7, s32[8,128]{1,0:T(8,128)} %bitcast.8, ...), custom_call_target="tpu_custom_call" | custom-call | tf_op jit(solution)/shard_map/distmult_step/pallas_call | solution.py:275
  80.3 3.1 %copy.11 = f32[1024,512]{1,0:T(8,128)} copy(f32[1024,512]{1,0:T(8,128)} %distmult_step.1) | data formatting | bytes 4194304

commit v2 on v1

v2 whole, which is shorter than its diff:
```python
import jax
import jax.numpy as jnp
from jax import lax
from jax.experimental import pallas as pl
from jax.experimental.pallas import tpu as pltpu
from jax.sharding import PartitionSpec as P

MESH = pl.DeviceIdType.MESH
CAP = 16
SLOTS = 2048
RELATION_PARTS = 8
GROUP = 16
GROUPS = 8
SPAN = CAP * GROUP
LANES = 128
F32 = jnp.float32
ROW_ORDER = (0, 1, 7, 6, 5, 4, 3, 2)


def partner_offsets():
    every = [(dx, dz, dy, dc) for dx in range(4) for dz in range(4) for dy in range(4) for dc in range(2)]
    hops = [sum(min(d, 4 - d) for d in o[:3]) for o in every]
    return [every[i] for i in sorted(range(len(every)), key=lambda i: (hops[i], i * 37 % 128))]


OFFSETS = partner_offsets()


def packed(digits):
    word = sum(d << (4 * i) for i, d in enumerate(digits))
    return word - (1 << 32) if word >= 1 << 31 else word


BF16 = jnp.bfloat16


def onehot(match):
    return jnp.where(match, 1.0, 0.0).astype(BF16)


def column(row):
    return jnp.transpose(jnp.broadcast_to(row, (LANES, LANES)))


def iota(shape, axis):
    return lax.broadcasted_iota(jnp.int32, shape, axis)


def kernel(
    table_h, rel_h, req_h, count_h, start_h, head_h, relid_h, tail_h, neg_h, offsets_h,
    out_ref,
    table, rel, req, count, start, look, relid, offsets,
    slotrow, slotcol, reqrow, lookcol, relwide, lookrow,
    idxbuf, wantrow, found, rows, rvec, emb, negb, qhalf, nweight, perrow, sent, back,
    local_sem, rel_sem, id_send, id_recv, row_send, row_recv, grad_send, grad_recv,
):
    w = lax.axis_index("wide")
    y = lax.axis_index("narrow")
    x, z, core = w // 8, (w // 2) % 4, w % 2

    xs, zs = [((x + d) & 3) * 8 for d in range(4)], [((z + d) & 3) * 2 + core for d in range(4)]
    ys, cores = [(y + d) & 3 for d in range(4)], [0, 1 - 2 * core]

    def partner(n):
        dx, dz, dy, dc = OFFSETS[n]
        return (xs[dx] + zs[dz] + cores[dc], ys[dy])

    def each_partner(g, sign, act):
        for u in range(GROUP):
            members = [OFFSETS[i * GROUP + u] for i in range(GROUPS)]
            xz = (packed([o[0] * 4 + o[1] for o in members]) >> (g * 4)) & 15
            yc = (packed([o[2] * 2 + o[3] for o in members]) >> (g * 4)) & 15
            px = (x + sign * (xz >> 2)) & 3
            pz = (z + sign * (xz & 3)) & 3
            py = (y + sign * (yc >> 1)) & 3
            device = (px * 8 + pz * 2 + ((core + yc) & 1), py)
            if u == 0:
                pl.when(g > 0)(lambda device=device: act(0, device))
            else:
                act(u, device)

    loads = [
        (start_h, start), (count_h, count), (req_h, req), (offsets_h, offsets), (table_h, table),
        (head_h, look.at[pl.ds(0, 8)]), (tail_h, look.at[pl.ds(8, 8)]), (neg_h, look.at[pl.ds(16, 8)]),
        (relid_h, relid),
    ]
    copies = [pltpu.make_async_copy(a, b, local_sem.at[i]) for i, (a, b) in enumerate(loads)]
    part = rel.shape[1]

    def load_relations(q):
        return pltpu.make_async_copy(
            rel_h.at[pl.ds(pl.multiple_of(q * part, part), part)], rel.at[q % 4], rel_sem.at[q % 4]
        )

    for copy in copies:
        copy.start()
    for q in range(4):
        load_relations(q).start()
    barrier = pltpu.get_barrier_semaphore()
    for n in range(GROUPS * GROUP - 1, 0, -1):
        pl.semaphore_signal(barrier, inc=1, device_id=partner(n), device_id_type=MESH)

    for copy in copies[:5]:
        copy.wait()

    row16 = iota((16, LANES), 0)
    first, many = start[...], count[...]
    facts = jnp.where(row16 == 0, first >> 6, jnp.where(row16 == 1, first & 63, jnp.where(row16 == 2, many, 0)))
    facts = facts.astype(F32).astype(BF16)
    asked = req[...]
    digits = jnp.concatenate([asked >> 5, asked & 31], axis=0).astype(F32).astype(BF16)
    lane = iota((1, SLOTS), 1)
    down = iota((LANES, SLOTS), 0)
    c = lane & 15
    off = offsets[...]
    ox, oz, oy, oc = off & 3, (off >> 2) & 3, (off >> 4) & 3, off >> 6
    owner = ((((x + ox) & 3) * 4 + ((z + oz) & 3)) * 2 + ((core + oc) & 1)) * 4 + ((y + oy) & 3)
    known = jnp.dot(facts, onehot(down == owner), preferred_element_type=F32)
    slot = (known[0:1] * 64.0 + known[1:2]).astype(jnp.int32) + c
    live = c < known[2:3].astype(jnp.int32)
    place = jnp.where(live, slot, -1).astype(F32)
    picked = jnp.dot(digits, onehot(down == (slot & 127)), preferred_element_type=F32)
    mine = iota((16, SLOTS), 0) == (slot >> 7)
    high = jnp.sum(jnp.where(mine, picked[:16], 0.0), axis=0, keepdims=True)
    low = jnp.sum(jnp.where(mine, picked[16:], 0.0), axis=0, keepdims=True)
    wanted = jnp.where(live, high * 32.0 + low, 0.0)
    for r in range(16):
        slotrow[r : r + 1] = place[:, r * LANES : (r + 1) * LANES]
        reqrow[r : r + 1] = wanted[:, r * LANES : (r + 1) * LANES]

    pl.semaphore_wait(barrier, GROUPS * GROUP - 1)

    for n in [g * GROUP + u for g in ROW_ORDER for u in range(GROUP)][1:]:
        pltpu.make_async_remote_copy(
            src_ref=reqrow.at[pl.ds(n // 8, 1)],
            dst_ref=idxbuf.at[pl.ds(n, 1)],
            send_sem=id_send,
            recv_sem=id_recv.at[n // GROUP],
            device_id=partner(n),
            device_id_type=MESH,
        ).start()

    idxbuf[0:1] = reqrow[0:1]

    some_device = partner(2)

    def arrived(buf, sem, g, unit):
        def wait(first, n):
            part = buf.at[pl.ds(pl.multiple_of(first * unit, unit), n * unit)]
            pltpu.make_async_remote_copy(
                src_ref=part, dst_ref=part, send_sem=sem.at[g], recv_sem=sem.at[g],
                device_id=some_device, device_id_type=MESH,
            ).wait_recv()

        pl.when(g == 0)(lambda: wait(1, GROUP - 1))
        pl.when(g > 0)(lambda: wait(g * GROUP, GROUP))

    def drained(buf, sem, unit):
        n = GROUPS * GROUP - 1
        part = buf.at[pl.ds(unit, n * unit)]
        pltpu.make_async_remote_copy(
            src_ref=part, dst_ref=part, send_sem=sem, recv_sem=sem, device_id=some_device, device_id_type=MESH
        ).wait_send()

    def send_blocks(src, dst, send_sem, recv_sem, g, sign):
        def send(u, device):
            at = pl.ds(pl.multiple_of((g * GROUP + u) * CAP, CAP), CAP)
            pltpu.make_async_remote_copy(
                src_ref=src.at[at], dst_ref=dst.at[at], send_sem=send_sem, recv_sem=recv_sem.at[g],
                device_id=device, device_id_type=MESH,
            ).start()

        each_partner(g, sign, send)

    for copy in copies[5:9]:
        copy.wait()
    lookrow[...] = look[...].astype(F32)

    def columns(dst, src, n):
        @pl.loop(0, n // 8)
        def _(i):
            for e in range(8):
                at = pl.ds(pl.multiple_of((i * 8 + e) * LANES, LANES), LANES)
                dst[at] = column(src[pl.ds(i * 8 + e, 1)])

    columns(lookcol, lookrow, 24)
    columns(slotcol, slotrow, 16)

    @pl.loop(0, GROUPS)
    def _(i):
        g = (packed(ROW_ORDER) >> (i * 4)) & 15
        arrived(idxbuf, id_recv, g, 1)
        belongs = (iota((8, LANES), 1) >> 4) == iota((8, LANES), 0)
        halves = []
        for h in range(2):
            got = idxbuf[pl.ds(pl.multiple_of(g * 16 + h * 8, 8), 8)]
            row = jnp.sum(jnp.where(belongs, got, 0.0), axis=0, keepdims=True)
            wantrow[pl.ds(g * 2 + h, 1)] = row
            halves.append(column(row).astype(jnp.int32))
        want = jnp.concatenate(halves, axis=0)
        across = iota((SPAN, LANES), 1)
        pick = jnp.concatenate([onehot(want == across + n * LANES) for n in range(8)], axis=1)
        here = jnp.dot(pick, table[...], preferred_element_type=F32).astype(BF16)
        found[pl.ds(pl.multiple_of(g * SPAN, SPAN), SPAN)] = here
        send_blocks(found, rows, row_send, row_recv, g, -1)

    rows[0:CAP] = found[0:CAP]

    @pl.loop(0, RELATION_PARTS)
    def _(q):
        load_relations(q).wait()
        for e in range(4):
            rows_at = pl.ds(pl.multiple_of(q * part + e * (part // 4), 8), part // 4)
            relwide[rows_at] = rel[q % 4, pl.ds(e * (part // 4), part // 4)].astype(F32)
        pl.when(q + 4 < RELATION_PARTS)(lambda: load_relations(q + 4).start())

    @pl.loop(0, rvec.shape[0] // 8)
    def _(i):
        for e in range(8):
            row = relid[i // 16, (i % 16) * 8 + e]
            rvec[pl.ds(i * 8 + e, 1)] = relwide[pl.ds(row, 1)]

    emb[...] = jnp.zeros_like(emb)

    @pl.loop(0, GROUPS)
    def _(i):
        g = (packed(ROW_ORDER) >> (i * 4)) & 15
        arrived(rows, row_recv, g, CAP)

        @pl.loop(0, 3)
        def _(b):
            at = pl.ds(pl.multiple_of(b * 1024, 1024), 1024)
            ids = lookcol[at]
            pick = jnp.concatenate([onehot(ids == slotrow[pl.ds(g * 2 + h, 1)]) for h in range(2)], axis=1)
            emb[at] += jnp.dot(pick, rows[pl.ds(pl.multiple_of(g * SPAN, SPAN), SPAN)], preferred_element_type=F32)

    negb[...] = emb[2048:].astype(BF16)

    @pl.loop(0, 4)
    def _(b):
        at = pl.ds(pl.multiple_of(b * 256, 256), 256)
        r = rvec[at]
        query = emb[at] * r
        half = query.astype(BF16)
        qhalf[at] = half
        tail = emb[pl.ds(pl.multiple_of(1024 + b * 256, 256), 256)]
        positive = jnp.sum(query * tail, axis=1, keepdims=True)
        pos_weight = -1.0 / (1.0 + jnp.exp(positive))
        perrow[pl.ds(pl.multiple_of(1024 + b * 256, 256), 256)] = (pos_weight * query).astype(BF16)
        score = lax.dot_general(half, negb[...], (((1,), (1,)), ((), ())), preferred_element_type=F32)
        weight = (1.0 / (1.0 + jnp.exp(-score))).astype(BF16)
        nweight[at] = weight
        pulled = jnp.dot(weight, negb[...], preferred_element_type=F32)
        perrow[at] = (r * (pos_weight * tail + pulled)).astype(BF16)

    perrow[2048:] = lax.dot_general(
        nweight[...], qhalf[...], (((0,), (0,)), ((), ())), preferred_element_type=F32
    ).astype(BF16)

    @pl.loop(0, GROUPS)
    def _(i):
        g = GROUPS - 1 - i
        at = pl.ds(pl.multiple_of(g * SPAN, SPAN), SPAN)
        place = slotcol[at]
        pick = jnp.concatenate([onehot(place == lookrow[n : n + 1]) for n in range(24)], axis=1)
        sent[at] = jnp.dot(pick, perrow[...], preferred_element_type=F32).astype(BF16)
        send_blocks(sent, back, grad_send, grad_recv, g, 1)

    back[0:CAP] = sent[0:CAP]
    out_ref[...] = jnp.zeros_like(out_ref)

    @pl.loop(0, GROUPS)
    def _(i):
        g = GROUPS - 1 - i
        arrived(back, grad_recv, g, CAP)
        down = iota((1024, LANES), 0).astype(F32)
        pick = jnp.concatenate([onehot(down == wantrow[pl.ds(g * 2 + h, 1)]) for h in range(2)], axis=1)
        out_ref[...] += jnp.dot(
            pick, back[pl.ds(pl.multiple_of(g * SPAN, SPAN), SPAN)], preferred_element_type=F32
        )

    drained(idxbuf, id_send, 1)
    drained(found, row_send, CAP)
    drained(sent, grad_send, CAP)


def per_device(table, relations, req_rows, owner_count, owner_start, head_slot, rel_id, tail_slot, neg_slot):
    ents, width = table.shape
    slots = req_rows.shape[1]
    batch = head_slot.shape[0]
    vmem = pltpu.VMEM
    dma = pltpu.SemaphoreType.DMA
    scratch = [
        vmem((ents, width), BF16), vmem((4, relations.shape[0] // RELATION_PARTS, width), BF16), vmem((16, LANES), jnp.int32),
        vmem((1, LANES), jnp.int32), vmem((1, LANES), jnp.int32), vmem((24, LANES), jnp.int32),
        pltpu.SMEM((8, LANES), jnp.int32), vmem((1, slots), jnp.int32),
        vmem((16, LANES), F32), vmem((slots, LANES), F32), vmem((16, LANES), F32),
        vmem((3 * batch, LANES), F32), vmem(relations.shape, F32), vmem((24, LANES), F32),
        vmem((128, LANES), F32), vmem((16, LANES), F32), vmem((slots, width), BF16), vmem((slots, width), BF16),
        vmem((batch, width), F32), vmem((3 * batch, width), F32), vmem((batch, width), BF16),
        vmem((batch, width), BF16), vmem((batch, batch), BF16), vmem((3 * batch, width), BF16),
        vmem((slots, width), BF16), vmem((slots, width), BF16),
        dma((9,)), dma((4,)), dma, dma((GROUPS,)), dma, dma((GROUPS,)), dma, dma((GROUPS,)),
    ]
    return pl.pallas_call(
        kernel,
        out_shape=jax.ShapeDtypeStruct((ents, width), F32),
        in_specs=[pl.BlockSpec(memory_space=pltpu.HBM)] * 10,
        out_specs=pl.BlockSpec(memory_space=pltpu.VMEM),
        scratch_shapes=scratch,
        compiler_params=pltpu.CompilerParams(
            collective_id=0, has_side_effects=True, vmem_limit_bytes=50 * 2**20
        ),
        name="distmult_step",
    )(*[pltpu.with_memory_space_constraint(v, pltpu.HBM) for v in (
        table,
        relations,
        req_rows.reshape(16, LANES),
        owner_count,
        owner_start,
        head_slot.reshape(8, LANES),
        rel_id.reshape(8, LANES),
        tail_slot.reshape(8, LANES),
        neg_slot.reshape(8, LANES),
        jnp.asarray([[o[0] | o[1] << 2 | o[2] << 4 | o[3] << 6 for o in OFFSETS for _ in range(CAP)]], jnp.int32),
    )])


def solution(mesh):
    both = ("wide", "narrow")
    in_specs = (P(both, None), P(), P(both, None), P(both, None), P(both, None), P(both), P(both), P(both), P(both))
    return jax.shard_map(per_device, mesh=mesh, in_specs=in_specs, out_specs=P(both, None), check_vma=False)
```

time: 83.5 us -> 78.3 us (0.938)
  Pallas kernels: 80.3 us -> 76.8 us
  local copies, waits for them, and re-layouts: 3.08 us -> 1.32 us
    pallas_call x1, Pallas kernels: 80.3 us -> 76.8 us  [per_device(): pl.pallas_call(kernel, out_shape=jax.ShapeDtypeStruct((ents, width), F32)...]
    unnamed x1, local copies, waits for them, and re-layouts: 3.08 us -> 1.32 us
where the time goes in v2:
time: 78.3 us; the launch traced here: 78.2 us
  Pallas kernels  76.8 us (98%)
  local copies, waits for them, and re-layouts  1.32 us (2%)
    pallas_call x1, Pallas kernels, per_device(): pl.pallas_call(kernel, out_shape=jax.ShapeDtypeStruct((ents, width), F32)...  76.8 us

profile of v2, /device:TPU:1, one launch (start us, length us, event | category | flops | bytes accessed | tf_op | source)
XLA Modules:
  0.0 78.2 jit_solution(16190119060995888305)
XLA Ops:
  0.0 76.8 %distmult_step.1 = f32[1024,512]{1,0:T(8,128)S(1)} custom-call(bf16[1024,512]{1,0:T(8,128)(2,1)} %table_h.1, bf16[7424,512]{1,0:T(8,128)(2,1)} %rel_h.1, s32[16,128]{1,0:T(8,128)} %bitcast.5, s32[1,128]{1,0:T(1,128)} %count_h.1, s32[1,128]{1,0:T(1,128)} %start_h.1, s32[8,128]{1,0:T(8,128)} %bitcast.6, s32[8,128]{1,0:T(8,128)} %bitcast.7, s32[8,128]{1,0:T(8,128)} %bitcast.8, ...), custom_call_target="tpu_custom_call" | custom-call | tf_op jit(solution)/shard_map/distmult_step/pallas_call | solution.py:305
  76.8 1.3 %copy.12 = f32[1024,512]{1,0:T(8,128)} copy(f32[1024,512]{1,0:T(8,128)S(1)} %distmult_step.1) | data formatting | bytes 4194304

commit v3 on v2

--- a/solution.py
+++ b/solution.py
@@ -14,13 +14,19 @@
 SPAN = CAP * GROUP
 LANES = 128
 F32 = jnp.float32
-ROW_ORDER = (0, 1, 7, 6, 5, 4, 3, 2)
+
+
+def hops(offset):
+    return sum(min(d, 4 - d) for d in offset[:3])
 
 
 def partner_offsets():
-    every = [(dx, dz, dy, dc) for dx in range(4) for dz in range(4) for dy in range(4) for dc in range(2)]
-    hops = [sum(min(d, 4 - d) for d in o[:3]) for o in every]
-    return [every[i] for i in sorted(range(len(every)), key=lambda i: (hops[i], i * 37 % 128))]
+    offsets = []
+    for g in range(GROUPS):
+        members = [(i // 4, i % 4, (g // 2 - i // 4 - i % 4) % 4, g % 2) for i in range(GROUP)]
+        members.sort(key=lambda o: (o != (0, 0, 0, 0), -hops(o)))
+        offsets += members
+    return offsets
 
 
 OFFSETS = partner_offsets()
@@ -65,8 +71,8 @@
         dx, dz, dy, dc = OFFSETS[n]
         return (xs[dx] + zs[dz] + cores[dc], ys[dy])
 
-    def each_partner(g, sign, act):
-        for u in range(GROUP):
+    def each_partner(g, half, sign, act):
+        for u in range(half * 8, half * 8 + 8):
             members = [OFFSETS[i * GROUP + u] for i in range(GROUPS)]
             xz = (packed([o[0] * 4 + o[1] for o in members]) >> (g * 4)) & 15
             yc = (packed([o[2] * 2 + o[3] for o in members]) >> (g * 4)) & 15
@@ -97,7 +103,7 @@
     for q in range(4):
         load_relations(q).start()
     barrier = pltpu.get_barrier_semaphore()
-    for n in range(GROUPS * GROUP - 1, 0, -1):
+    for n in sorted(range(1, GROUPS * GROUP), key=lambda n: -hops(OFFSETS[n])):
         pl.semaphore_signal(barrier, inc=1, device_id=partner(n), device_id_type=MESH)
 
     for copy in copies[:5]:
@@ -130,7 +136,7 @@
 
     pl.semaphore_wait(barrier, GROUPS * GROUP - 1)
 
-    for n in [g * GROUP + u for g in ROW_ORDER for u in range(GROUP)][1:]:
+    for n in range(1, GROUPS * GROUP):
         pltpu.make_async_remote_copy(
             src_ref=reqrow.at[pl.ds(n // 8, 1)],
             dst_ref=idxbuf.at[pl.ds(n, 1)],
@@ -162,7 +168,7 @@
             src_ref=part, dst_ref=part, send_sem=sem, recv_sem=sem, device_id=some_device, device_id_type=MESH
         ).wait_send()
 
-    def send_blocks(src, dst, send_sem, recv_sem, g, sign):
+    def send_blocks(src, dst, send_sem, recv_sem, g, half, sign):
         def send(u, device):
             at = pl.ds(pl.multiple_of((g * GROUP + u) * CAP, CAP), CAP)
             pltpu.make_async_remote_copy(
@@ -170,7 +176,7 @@
                 device_id=device, device_id_type=MESH,
             ).start()
 
-        each_partner(g, sign, send)
+        each_partner(g, half, sign, send)
 
     for copy in copies[5:9]:
         copy.wait()
@@ -187,22 +193,19 @@
     columns(slotcol, slotrow, 16)
 
     @pl.loop(0, GROUPS)
-    def _(i):
-        g = (packed(ROW_ORDER) >> (i * 4)) & 15
+    def _(g):
         arrived(idxbuf, id_recv, g, 1)
         belongs = (iota((8, LANES), 1) >> 4) == iota((8, LANES), 0)
-        halves = []
-        for h in range(2):
-            got = idxbuf[pl.ds(pl.multiple_of(g * 16 + h * 8, 8), 8)]
+        across = iota((LANES, LANES), 1)
+        for half in range(2):
+            got = idxbuf[pl.ds(pl.multiple_of(g * 16 + half * 8, 8), 8)]
             row = jnp.sum(jnp.where(belongs, got, 0.0), axis=0, keepdims=True)
-            wantrow[pl.ds(g * 2 + h, 1)] = row
-            halves.append(column(row).astype(jnp.int32))
-        want = jnp.concatenate(halves, axis=0)
-        across = iota((SPAN, LANES), 1)
-        pick = jnp.concatenate([onehot(want == across + n * LANES) for n in range(8)], axis=1)
-        here = jnp.dot(pick, table[...], preferred_element_type=F32).astype(BF16)
-        found[pl.ds(pl.multiple_of(g * SPAN, SPAN), SPAN)] = here
-        send_blocks(found, rows, row_send, row_recv, g, -1)
+            wantrow[pl.ds(g * 2 + half, 1)] = row
+            want = column(row).astype(jnp.int32)
+            pick = jnp.concatenate([onehot(want == across + n * LANES) for n in range(8)], axis=1)
+            here = jnp.dot(pick, table[...], preferred_element_type=F32).astype(BF16)
+            found[pl.ds(pl.multiple_of(g * SPAN + half * LANES, LANES), LANES)] = here
+            send_blocks(found, rows, row_send, row_recv, g, half, -1)
 
     rows[0:CAP] = found[0:CAP]
 
@@ -223,8 +226,7 @@
     emb[...] = jnp.zeros_like(emb)
 
     @pl.loop(0, GROUPS)
-    def _(i):
-        g = (packed(ROW_ORDER) >> (i * 4)) & 15
+    def _(g):
         arrived(rows, row_recv, g, CAP)
 
         @pl.loop(0, 3)
@@ -236,17 +238,16 @@
 
     negb[...] = emb[2048:].astype(BF16)
 
-    @pl.loop(0, 4)
-    def _(b):
-        at = pl.ds(pl.multiple_of(b * 256, 256), 256)
+    for b in range(4):
+        at, tail_at = pl.ds(b * 256, 256), pl.ds(1024 + b * 256, 256)
         r = rvec[at]
         query = emb[at] * r
         half = query.astype(BF16)
         qhalf[at] = half
-        tail = emb[pl.ds(pl.multiple_of(1024 + b * 256, 256), 256)]
+        tail = emb[tail_at]
         positive = jnp.sum(query * tail, axis=1, keepdims=True)
         pos_weight = -1.0 / (1.0 + jnp.exp(positive))
-        perrow[pl.ds(pl.multiple_of(1024 + b * 256, 256), 256)] = (pos_weight * query).astype(BF16)
+        perrow[tail_at] = (pos_weight * query).astype(BF16)
         score = lax.dot_general(half, negb[...], (((1,), (1,)), ((), ())), preferred_element_type=F32)
         weight = (1.0 / (1.0 + jnp.exp(-score))).astype(BF16)
         nweight[at] = weight
@@ -260,11 +261,12 @@
     @pl.loop(0, GROUPS)
     def _(i):
         g = GROUPS - 1 - i
-        at = pl.ds(pl.multiple_of(g * SPAN, SPAN), SPAN)
-        place = slotcol[at]
-        pick = jnp.concatenate([onehot(place == lookrow[n : n + 1]) for n in range(24)], axis=1)
-        sent[at] = jnp.dot(pick, perrow[...], preferred_element_type=F32).astype(BF16)
-        send_blocks(sent, back, grad_send, grad_recv, g, 1)
+        for half in range(2):
+            at = pl.ds(pl.multiple_of(g * SPAN + half * LANES, LANES), LANES)
+            place = slotcol[at]
+            pick = jnp.concatenate([onehot(place == lookrow[n : n + 1]) for n in range(24)], axis=1)
+            sent[at] = jnp.dot(pick, perrow[...], preferred_element_type=F32).astype(BF16)
+            send_blocks(sent, back, grad_send, grad_recv, g, half, 1)
 
     back[0:CAP] = sent[0:CAP]
     out_ref[...] = jnp.zeros_like(out_ref)

time: 78.3 us -> 75.8 us (0.968)
  Pallas kernels: 76.8 us -> 74.4 us
    pallas_call x1, Pallas kernels: 76.8 us -> 74.4 us  [per_device(): pl.pallas_call(kernel, out_shape=jax.ShapeDtypeStruct((ents, width), F32)...]
where the time goes in v3:
time: 75.8 us; the launch traced here: 75.7 us
  Pallas kernels  74.4 us (98%)
  local copies, waits for them, and re-layouts  1.32 us (2%)
    pallas_call x1, Pallas kernels, per_device(): pl.pallas_call(kernel, out_shape=jax.ShapeDtypeStruct((ents, width), F32)...  74.4 us

profile of v3, /device:TPU:1, one launch (start us, length us, event | category | flops | bytes accessed | tf_op | source)
XLA Modules:
  0.0 75.7 jit_solution(1851875009792438482)
XLA Ops:
  0.0 74.4 %distmult_step.1 = f32[1024,512]{1,0:T(8,128)S(1)} custom-call(bf16[1024,512]{1,0:T(8,128)(2,1)} %table_h.1, bf16[7424,512]{1,0:T(8,128)(2,1)} %rel_h.1, s32[16,128]{1,0:T(8,128)} %bitcast.5, s32[1,128]{1,0:T(1,128)} %count_h.1, s32[1,128]{1,0:T(1,128)} %start_h.1, s32[8,128]{1,0:T(8,128)} %bitcast.6, s32[8,128]{1,0:T(8,128)} %bitcast.7, s32[8,128]{1,0:T(8,128)} %bitcast.8, ...), custom_call_target="tpu_custom_call" | custom-call | tf_op jit(solution)/shard_map/distmult_step/pallas_call | solution.py:307
  74.4 1.3 %copy.12 = f32[1024,512]{1,0:T(8,128)} copy(f32[1024,512]{1,0:T(8,128)S(1)} %distmult_step.1) | data formatting | bytes 4194304

commit v4 on v3

--- a/solution.py
+++ b/solution.py
@@ -57,7 +57,7 @@
     out_ref,
     table, rel, req, count, start, look, relid, offsets,
     slotrow, slotcol, reqrow, lookcol, relwide, lookrow,
-    idxbuf, wantrow, found, rows, rvec, emb, negb, qhalf, nweight, perrow, sent, back,
+    idxbuf, wantrow, found, rows, rvec, emb, negb, perrow, sent, back,
     local_sem, rel_sem, id_send, id_recv, row_send, row_recv, grad_send, grad_recv,
 ):
     w = lax.axis_index("wide")
@@ -141,7 +141,7 @@
             src_ref=reqrow.at[pl.ds(n // 8, 1)],
             dst_ref=idxbuf.at[pl.ds(n, 1)],
             send_sem=id_send,
-            recv_sem=id_recv.at[n // GROUP],
+            recv_sem=id_recv.at[n // 8],
             device_id=partner(n),
             device_id_type=MESH,
         ).start()
@@ -150,16 +150,20 @@
 
     some_device = partner(2)
 
-    def arrived(buf, sem, g, unit):
+    def arrived(buf, sem, g, blocks, unit):
         def wait(first, n):
-            part = buf.at[pl.ds(pl.multiple_of(first * unit, unit), n * unit)]
+            at = first * unit if isinstance(first, int) else pl.multiple_of(first * unit, unit)
+            part = buf.at[pl.ds(at, n * unit)]
             pltpu.make_async_remote_copy(
                 src_ref=part, dst_ref=part, send_sem=sem.at[g], recv_sem=sem.at[g],
                 device_id=some_device, device_id_type=MESH,
             ).wait_recv()
 
-        pl.when(g == 0)(lambda: wait(1, GROUP - 1))
-        pl.when(g > 0)(lambda: wait(g * GROUP, GROUP))
+        if isinstance(g, int):
+            wait(g * blocks + (g == 0), blocks - (g == 0))
+        else:
+            pl.when(g == 0)(lambda: wait(1, blocks - 1))
+            pl.when(g > 0)(lambda: wait(g * blocks, blocks))
 
     def drained(buf, sem, unit):
         n = GROUPS * GROUP - 1
@@ -172,7 +176,7 @@
         def send(u, device):
             at = pl.ds(pl.multiple_of((g * GROUP + u) * CAP, CAP), CAP)
             pltpu.make_async_remote_copy(
-                src_ref=src.at[at], dst_ref=dst.at[at], send_sem=send_sem, recv_sem=recv_sem.at[g],
+                src_ref=src.at[at], dst_ref=dst.at[at], send_sem=send_sem, recv_sem=recv_sem.at[g * 2 + half],
                 device_id=device, device_id_type=MESH,
             ).start()
 
@@ -192,12 +196,18 @@
     columns(lookcol, lookrow, 24)
     columns(slotcol, slotrow, 16)
 
+    def widen_relations(q):
+        load_relations(q).wait()
+        for e in range(4):
+            rows_at = pl.ds(pl.multiple_of(q * part + e * (part // 4), 8), part // 4)
+            relwide[rows_at] = rel[q % 4, pl.ds(e * (part // 4), part // 4)].astype(F32)
+
     @pl.loop(0, GROUPS)
     def _(g):
-        arrived(idxbuf, id_recv, g, 1)
         belongs = (iota((8, LANES), 1) >> 4) == iota((8, LANES), 0)
         across = iota((LANES, LANES), 1)
         for half in range(2):
+            arrived(idxbuf, id_recv, g * 2 + half, 8, 1)
             got = idxbuf[pl.ds(pl.multiple_of(g * 16 + half * 8, 8), 8)]
             row = jnp.sum(jnp.where(belongs, got, 0.0), axis=0, keepdims=True)
             wantrow[pl.ds(g * 2 + half, 1)] = row
@@ -211,52 +221,55 @@
 
     @pl.loop(0, RELATION_PARTS)
     def _(q):
-        load_relations(q).wait()
-        for e in range(4):
-            rows_at = pl.ds(pl.multiple_of(q * part + e * (part // 4), 8), part // 4)
-            relwide[rows_at] = rel[q % 4, pl.ds(e * (part // 4), part // 4)].astype(F32)
+        widen_relations(q)
         pl.when(q + 4 < RELATION_PARTS)(lambda: load_relations(q + 4).start())
 
-    @pl.loop(0, rvec.shape[0] // 8)
+    @pl.loop(0, rvec.shape[0] // 32)
     def _(i):
-        for e in range(8):
-            row = relid[i // 16, (i % 16) * 8 + e]
-            rvec[pl.ds(i * 8 + e, 1)] = relwide[pl.ds(row, 1)]
+        for e in range(32):
+            row = relid[i // 4, (i % 4) * 32 + e]
+            rvec[pl.ds(i * 32 + e, 1)] = relwide[pl.ds(row, 1)]
 
     emb[...] = jnp.zeros_like(emb)
 
-    @pl.loop(0, GROUPS)
-    def _(g):
-        arrived(rows, row_recv, g, CAP)
+    def gather_slots(first, halves):
+        for h in range(halves):
+            arrived(rows, row_recv, first + h, 8, CAP)
 
         @pl.loop(0, 3)
         def _(b):
             at = pl.ds(pl.multiple_of(b * 1024, 1024), 1024)
             ids = lookcol[at]
-            pick = jnp.concatenate([onehot(ids == slotrow[pl.ds(g * 2 + h, 1)]) for h in range(2)], axis=1)
-            emb[at] += jnp.dot(pick, rows[pl.ds(pl.multiple_of(g * SPAN, SPAN), SPAN)], preferred_element_type=F32)
+            places = [slotrow[pl.ds(first + h, 1)] for h in range(halves)]
+            pick = jnp.concatenate([onehot(ids == place) for place in places], axis=1)
+            span = rows[pl.ds(first * LANES, halves * LANES)]
+            emb[at] += jnp.dot(pick, span, preferred_element_type=F32)
+
+    for half, halves in ((0, 4), (4, 4), (8, 2), (10, 2), (12, 2), (14, 2)):
+        gather_slots(half, halves)
 
     negb[...] = emb[2048:].astype(BF16)
 
-    for b in range(4):
-        at, tail_at = pl.ds(b * 256, 256), pl.ds(1024 + b * 256, 256)
+    for b in range(2):
+        at, tail_at = pl.ds(b * 512, 512), pl.ds(1024 + b * 512, 512)
         r = rvec[at]
         query = emb[at] * r
         half = query.astype(BF16)
-        qhalf[at] = half
         tail = emb[tail_at]
         positive = jnp.sum(query * tail, axis=1, keepdims=True)
         pos_weight = -1.0 / (1.0 + jnp.exp(positive))
         perrow[tail_at] = (pos_weight * query).astype(BF16)
         score = lax.dot_general(half, negb[...], (((1,), (1,)), ((), ())), preferred_element_type=F32)
         weight = (1.0 / (1.0 + jnp.exp(-score))).astype(BF16)
-        nweight[at] = weight
         pulled = jnp.dot(weight, negb[...], preferred_element_type=F32)
         perrow[at] = (r * (pos_weight * tail + pulled)).astype(BF16)
-
-    perrow[2048:] = lax.dot_general(
-        nweight[...], qhalf[...], (((0,), (0,)), ((), ())), preferred_element_type=F32
-    ).astype(BF16)
+        pushed = lax.dot_general(weight, half, (((0,), (0,)), ((), ())), preferred_element_type=F32)
+        if b == 0:
+            emb[2048:] = pushed
+        elif b < 1:
+            emb[2048:] += pushed
+        else:
+            perrow[2048:] = (emb[2048:] + pushed).astype(BF16)
 
     @pl.loop(0, GROUPS)
     def _(i):
@@ -271,15 +284,12 @@
     back[0:CAP] = sent[0:CAP]
     out_ref[...] = jnp.zeros_like(out_ref)
 
-    @pl.loop(0, GROUPS)
-    def _(i):
-        g = GROUPS - 1 - i
-        arrived(back, grad_recv, g, CAP)
+    for i in range(2 * GROUPS):
+        h = 2 * (GROUPS - 1 - i // 2) + i % 2
+        arrived(back, grad_recv, h, 8, CAP)
         down = iota((1024, LANES), 0).astype(F32)
-        pick = jnp.concatenate([onehot(down == wantrow[pl.ds(g * 2 + h, 1)]) for h in range(2)], axis=1)
-        out_ref[...] += jnp.dot(
-            pick, back[pl.ds(pl.multiple_of(g * SPAN, SPAN), SPAN)], preferred_element_type=F32
-        )
+        pick = onehot(down == wantrow[h : h + 1])
+        out_ref[...] += jnp.dot(pick, back[h * LANES : (h + 1) * LANES], preferred_element_type=F32)
 
     drained(idxbuf, id_send, 1)
     drained(found, row_send, CAP)
@@ -300,9 +310,9 @@
         vmem((3 * batch, LANES), F32), vmem(relations.shape, F32), vmem((24, LANES), F32),
         vmem((128, LANES), F32), vmem((16, LANES), F32), vmem((slots, width), BF16), vmem((slots, width), BF16),
         vmem((batch, width), F32), vmem((3 * batch, width), F32), vmem((batch, width), BF16),
-        vmem((batch, width), BF16), vmem((batch, batch), BF16), vmem((3 * batch, width), BF16),
+        vmem((3 * batch, width), BF16),
         vmem((slots, width), BF16), vmem((slots, width), BF16),
-        dma((9,)), dma((4,)), dma, dma((GROUPS,)), dma, dma((GROUPS,)), dma, dma((GROUPS,)),
+        dma((9,)), dma((4,)), dma, dma((2 * GROUPS,)), dma, dma((2 * GROUPS,)), dma, dma((2 * GROUPS,)),
     ]
     return pl.pallas_call(
         kernel,

time: 75.8 us -> 75.5 us (level)
  no operation moved by 1% of the time
where the time goes in v4:
time: 75.5 us; the launch traced here: 75.3 us
  Pallas kernels  74 us (98%)
  local copies, waits for them, and re-layouts  1.32 us (2%)
    pallas_call x1, Pallas kernels, per_device(): pl.pallas_call(kernel, out_shape=jax.ShapeDtypeStruct((ents, width), F32)...  74 us

profile of v4, /device:TPU:1, one launch (start us, length us, event | category | flops | bytes accessed | tf_op | source)
XLA Modules:
  0.0 75.3 jit_solution(1187776159148899467)
XLA Ops:
  0.0 74.0 %distmult_step.1 = f32[1024,512]{1,0:T(8,128)S(1)} custom-call(bf16[1024,512]{1,0:T(8,128)(2,1)} %table_h.1, bf16[7424,512]{1,0:T(8,128)(2,1)} %rel_h.1, s32[16,128]{1,0:T(8,128)} %bitcast.5, s32[1,128]{1,0:T(1,128)} %count_h.1, s32[1,128]{1,0:T(1,128)} %start_h.1, s32[8,128]{1,0:T(8,128)} %bitcast.6, s32[8,128]{1,0:T(8,128)} %bitcast.7, s32[8,128]{1,0:T(8,128)} %bitcast.8, ...), custom_call_target="tpu_custom_call" | custom-call | tf_op jit(solution)/shard_map/distmult_step/pallas_call | solution.py:317
  74.0 1.3 %copy.12 = f32[1024,512]{1,0:T(8,128)} copy(f32[1024,512]{1,0:T(8,128)S(1)} %distmult_step.1) | data formatting | bytes 4194304

commit v5 on v4

--- a/solution.py
+++ b/solution.py
@@ -98,15 +98,17 @@
             rel_h.at[pl.ds(pl.multiple_of(q * part, part), part)], rel.at[q % 4], rel_sem.at[q % 4]
         )
 
-    for copy in copies:
+    for copy in copies[:5]:
+        copy.start()
+    barrier = pltpu.get_barrier_semaphore()
+    for n in sorted(range(1, GROUPS * GROUP), key=lambda n: -hops(OFFSETS[n])):
+        pl.semaphore_signal(barrier, inc=1, device_id=partner(n), device_id_type=MESH)
+
+    for copy in copies[5:]:
         copy.start()
     for q in range(4):
         load_relations(q).start()
-    barrier = pltpu.get_barrier_semaphore()
-    for n in sorted(range(1, GROUPS * GROUP), key=lambda n: -hops(OFFSETS[n])):
-        pl.semaphore_signal(barrier, inc=1, device_id=partner(n), device_id_type=MESH)
-
-    for copy in copies[:5]:
+    for copy in copies[:4]:
         copy.wait()
 
     row16 = iota((16, LANES), 0)
@@ -182,7 +184,7 @@
 
         each_partner(g, half, sign, send)
 
-    for copy in copies[5:9]:
+    for copy in copies[4:9]:
         copy.wait()
     lookrow[...] = look[...].astype(F32)
 
@@ -236,19 +238,26 @@
         for h in range(halves):
             arrived(rows, row_recv, first + h, 8, CAP)
 
-        @pl.loop(0, 3)
-        def _(b):
-            at = pl.ds(pl.multiple_of(b * 1024, 1024), 1024)
+        def found_in(at):
             ids = lookcol[at]
             places = [slotrow[pl.ds(first + h, 1)] for h in range(halves)]
             pick = jnp.concatenate([onehot(ids == place) for place in places], axis=1)
             span = rows[pl.ds(first * LANES, halves * LANES)]
-            emb[at] += jnp.dot(pick, span, preferred_element_type=F32)
+            return emb[at] + jnp.dot(pick, span, preferred_element_type=F32)
+
+        last = first + halves == 2 * GROUPS
+
+        @pl.loop(0, 2 if last else 3)
+        def _(b):
+            at = pl.ds(pl.multiple_of(b * 1024, 1024), 1024)
+            emb[at] = found_in(at)
+
+        if last:
+            negb[...] = found_in(pl.ds(2048, 1024)).astype(BF16)
 
     for half, halves in ((0, 4), (4, 4), (8, 2), (10, 2), (12, 2), (14, 2)):
         gather_slots(half, halves)
 
-    negb[...] = emb[2048:].astype(BF16)
 
     for b in range(2):
         at, tail_at = pl.ds(b * 512, 512), pl.ds(1024 + b * 512, 512)

time: 75.5 us -> 75.5 us (level)
  no operation moved by 1% of the time
where the time goes in v5:
time: 75.5 us; the launch traced here: 75.3 us
  Pallas kernels  74 us (98%)
  local copies, waits for them, and re-layouts  1.32 us (2%)
    pallas_call x1, Pallas kernels, per_device(): pl.pallas_call(kernel, out_shape=jax.ShapeDtypeStruct((ents, width), F32)...  74 us

profile of v5, /device:TPU:1, one launch (start us, length us, event | category | flops | bytes accessed | tf_op | source)
XLA Modules:
  0.0 75.3 jit_solution(17013954293280964840)
XLA Ops:
  0.0 74.0 %distmult_step.1 = f32[1024,512]{1,0:T(8,128)S(1)} custom-call(bf16[1024,512]{1,0:T(8,128)(2,1)} %table_h.1, bf16[7424,512]{1,0:T(8,128)(2,1)} %rel_h.1, s32[16,128]{1,0:T(8,128)} %bitcast.5, s32[1,128]{1,0:T(1,128)} %count_h.1, s32[1,128]{1,0:T(1,128)} %start_h.1, s32[8,128]{1,0:T(8,128)} %bitcast.6, s32[8,128]{1,0:T(8,128)} %bitcast.7, s32[8,128]{1,0:T(8,128)} %bitcast.8, ...), custom_call_target="tpu_custom_call" | custom-call | tf_op jit(solution)/shard_map/distmult_step/pallas_call | solution.py:326
  74.0 1.3 %copy.12 = f32[1024,512]{1,0:T(8,128)} copy(f32[1024,512]{1,0:T(8,128)S(1)} %distmult_step.1) | data formatting | bytes 4194304
